TPU v7x, 32 devices: a whole 2x2x4 slice. The times are simulated.
32 devices in a mesh: groups: 2 (over y), gx: 16 (over z, x, core).
Axes of the slice: x: 2, y: 2, z: 4, core: 2. Of those that a mesh axis runs over, the one named last changes fastest.
Arguments:
- pressure: float32 [7, 256, 128, 128], P(None, ('groups', 'gx')), parts along dimension 1, may hold values from -6 to 6
- adjoint: float32 [7, 256, 128, 128], P(None, ('groups', 'gx')), parts along dimension 1, may hold values from -6 to 6
- permeability: float32 [3, 256, 128, 128], P(None, ('groups', 'gx')), parts along dimension 1, may hold values from 0.02 to 40, as said below
- active: int32 [256, 128, 128], P(('groups', 'gx')), parts along dimension 0, may hold values 0 or 1
- fault_codes: int32 [3, 256, 128, 128], P(None, ('groups', 'gx')), parts along dimension 1, may hold values from 0 to 3
Outputs:
- gradient: float32 [3, 256, 128, 128], P(None, ('groups', 'gx')), parts along dimension 1
There are 2 independent parts, one for each index of `groups`. A program takes and returns all parts, laid end to end along the dimension named above; each array names one. Nothing has to cross between parts.
Inputs may be any that keep to these rules, and one draw needn't show every extreme that they name: `permeability`: Positive.
All inputs are finite; a program needn't handle non-finite values. No bound on the sum of `active` on one device may be relied on, other than what follows from the above.
Results may differ from a plain program's by a relative error of at most 0.0003.
Values sent between devices are 32-bit elements; how exact they have to be, the bound alone decides.
A program may use at most 64 MiB of HBM per device.

v0:
```python
import functools

import jax
import jax.numpy as jnp
from jax import lax
from jax.experimental import pallas as pl
from jax.experimental.pallas import tpu as pltpu
from jax.sharding import PartitionSpec as P

MESH = pl.DeviceIdType.MESH
epsilon = 1e-06
ROWS = 32
PAD = 8
GRANT = 58_000_000


def multiplier(codes):
    return jnp.where(codes == 0, 1.0, jnp.where(codes == 1, 0.6, jnp.where(codes == 2, 0.25, 0.05))).astype(jnp.float32)


def fold(values):
    squares = values * values
    total = squares[0:8]
    for i in range(8, squares.shape[0], 8):
        total = total + squares[i : i + 8]
    return total


def weight(products, factor, k_lo, k_up):
    summed = k_lo + k_up
    return 2.0 * factor * products * (k_lo * k_up) / (summed * summed)


def distances(n):
    reach, rounds = 1, []
    while reach < n - 1:
        rounds.append(reach)
        reach *= 2
    return rounds


def kernel(
    n, entries, p_hbm, a_hbm, k_hbm, act_hbm, code_hbm, grad,
    p, a, k, act, code, halo_p, halo_a, halo_g, halo_own, g_out, ret_out, ret_in, tail, acc, part, parts,
    load_sem, halo_send, halo_recv, ret_send, ret_recv, part_send, part_recv, near_sem,
):
    me = lax.axis_index("gx")
    lower, upper = me - 1, me + 1
    steps, layers, height, width = p_hbm.shape
    last = layers - 1
    blocks = height // ROWS

    barrier = pltpu.get_barrier_semaphore()

    def signal(semaphore, distance):
        for there, inside in ((me - distance, me >= distance), (me + distance, me + distance < n)):
            @pl.when(inside)
            def _():
                pl.semaphore_signal(semaphore, inc=1, device_id={"gx": there}, device_id_type=MESH)

    def await_signals(semaphore, distance):
        peers = jnp.where(me >= distance, 1, 0) + jnp.where(me + distance < n, 1, 0)
        pl.semaphore_wait(semaphore, peers)

    @pl.when(upper < n)
    def _():
        pl.semaphore_signal(barrier, inc=1, device_id={"gx": upper}, device_id_type=MESH)

    rounds = distances(n)

    def turn(i):
        if i > 0:
            await_signals(near_sem.at[i - 1], rounds[i - 1])
        else:
            @pl.when(upper < n)
            def _():
                pl.semaphore_wait(near_sem.at[len(rounds)], 1)

        if i < len(rounds):
            signal(near_sem.at[i], rounds[i])

    def loads(l):
        return (
            pltpu.make_async_copy(k_hbm.at[:, l], k.at[:, l, pl.ds(0, height)], load_sem.at[2, l]),
            pltpu.make_async_copy(act_hbm.at[l], act.at[l, pl.ds(0, height)], load_sem.at[3, l]),
            pltpu.make_async_copy(code_hbm.at[:, l], code.at[:, l], load_sem.at[4, l]),
            pltpu.make_async_copy(p_hbm.at[:, l], p.at[:, l, pl.ds(0, height)], load_sem.at[0, l]),
            pltpu.make_async_copy(a_hbm.at[:, l], a.at[:, l, pl.ds(0, height)], load_sem.at[1, l]),
        )

    def halo_pa(c):
        rows = pl.ds(c * ROWS, ROWS)
        return (
            pltpu.make_async_remote_copy(
                src_ref=p_hbm.at[:, 0, rows], dst_ref=halo_p.at[:, rows],
                send_sem=halo_send.at[2 * c], recv_sem=halo_recv.at[2 * c],
                device_id={"gx": lower}, device_id_type=MESH),
            pltpu.make_async_remote_copy(
                src_ref=a_hbm.at[:, 0, rows], dst_ref=halo_a.at[:, rows],
                send_sem=halo_send.at[2 * c + 1], recv_sem=halo_recv.at[2 * c + 1],
                device_id={"gx": lower}, device_id_type=MESH),
        )

    halo_k = pltpu.make_async_remote_copy(
        src_ref=g_out, dst_ref=halo_g, send_sem=halo_send.at[2 * blocks], recv_sem=halo_recv.at[2 * blocks],
        device_id={"gx": lower}, device_id_type=MESH)

    halo_first = pltpu.make_async_remote_copy(
        src_ref=grad.at[0, 0, pl.ds(height - ROWS, ROWS)], dst_ref=halo_own, send_sem=halo_send.at[2 * blocks + 1], recv_sem=halo_recv.at[2 * blocks + 1],
        device_id={"gx": lower}, device_id_type=MESH)

    def returned(c):
        rows = pl.ds(c * ROWS, ROWS)
        return pltpu.make_async_remote_copy(
            src_ref=ret_out.at[rows], dst_ref=ret_in.at[rows], send_sem=ret_send.at[c], recv_sem=ret_recv.at[c],
            device_id={"gx": upper}, device_id_type=MESH)

    first = loads(0)
    for copy in first[:3]:
        copy.start()

    @pl.when(me > 0)
    def _():
        pl.semaphore_wait(barrier, 1)
        pl.semaphore_signal(near_sem.at[len(rounds)], inc=1, device_id={"gx": lower}, device_id_type=MESH)


    @pl.when(me > 0)
    def _():
        for c in range(blocks // 2):
            for copy in halo_pa(c):
                copy.start()

    for copy in first[3:]:
        copy.start()

    def start_layer(l, carry):
        for copy in loads(l):
            copy.start()
        return carry

    lax.fori_loop(1, layers, start_layer, 0)
    for copy in first[:2]:
        copy.wait()
    g_out[...] = k[0, 0, 0:height] * act[0, 0:height].astype(jnp.float32)

    @pl.when(me > 0)
    def _():
        halo_k.start()

    for copy in first[2:]:
        copy.wait()
    tail[0:8] = jnp.zeros((8, width), jnp.float32)
    lane = lax.broadcasted_iota(jnp.int32, (ROWS, width), 1)
    row = lax.broadcasted_iota(jnp.int32, (ROWS, width), 0)
    grad[0, 0] = jnp.zeros((height, width), jnp.float32)

    def layer(l, total):
        @pl.when(l < last)
        def _():
            for copy in loads(l + 1):
                copy.wait()

        @pl.when(jnp.logical_and(l == 1, me > 0))
        def _():
            halo_first.start()
            for c in range(blocks // 2, blocks):
                for copy in halo_pa(c):
                    copy.start()

        for i in range(0, min(layers - 1, len(rounds) + 1)):
            @pl.when(l == i + 1)
            def _(i=i):
                turn(i)

        def block(b, total):
            r = pl.multiple_of(b * ROWS, ROWS)
            here, after = pl.ds(r, ROWS), pl.ds(r + 1, ROWS)
            prod_y = jnp.zeros((ROWS, width), jnp.float32)
            prod_z = jnp.zeros((ROWS, width), jnp.float32)
            for t in range(steps):
                pt, at = p[t, l, here], a[t, l, here]
                prod_y += (at - a[t, l, after]) * (pt - p[t, l, after])
                prod_z += (at - pltpu.roll(at, width - 1, 1)) * (pt - pltpu.roll(pt, width - 1, 1))
            opened = act[l, here].astype(jnp.float32)
            k1 = k[1, l, here]
            k1_up = k[1, l, after]
            factor = multiplier(code[1, l, here]) * opened * act[l, after].astype(jnp.float32)
            w = jnp.where(row + r < height - 1, weight(prod_y, factor, k1, k1_up), 0.0)
            w_lo = jnp.where(row + r < height - 1, w * k1_up, 0.0)
            tail[pl.ds(r + 8, ROWS)] = w * k1
            log1 = w_lo + tail[pl.ds(r + 7, ROWS)]
            grad[1, l, here] = log1
            k2 = k[2, l, here]
            k2_up = pltpu.roll(k2, width - 1, 1)
            factor = multiplier(code[2, l, here]) * opened * pltpu.roll(opened, width - 1, 1)
            w = jnp.where(lane < width - 1, weight(prod_z, factor, k2, k2_up), 0.0)
            log2 = w * k2_up + pltpu.roll(w * k2, 1, 1)
            grad[2, l, here] = log2
            return total + fold(log1) + fold(log2)

        total = lax.fori_loop(0, blocks, block, total)

        def cross(b, total):
            here = pl.ds(pl.multiple_of(b * ROWS, ROWS), ROWS)
            prod = jnp.zeros((ROWS, width), jnp.float32)
            for t in range(steps):
                prod += (a[t, l, here] - a[t, l + 1, here]) * (p[t, l, here] - p[t, l + 1, here])
            k0, k0_up = k[0, l, here], k[0, l + 1, here]
            factor = multiplier(code[0, l, here]) * (act[l, here] * act[l + 1, here]).astype(jnp.float32)
            w = weight(prod, factor, k0, k0_up)
            log0 = grad[0, l, here] + w * k0_up
            grad[0, l, here] = log0
            grad[0, l + 1, here] = w * k0
            return total + jnp.where(l > 0, 1.0, 0.0) * fold(log0)

        return lax.cond(l < last, lambda total: lax.fori_loop(0, blocks, cross, total), lambda total: total, total)

    total = lax.fori_loop(0, layers, layer, jnp.zeros((8, width), jnp.float32))
    for i in range(layers - 1, len(rounds) + 1):
        turn(i)

    acc[...] = total + jnp.where(me == 0, 1.0, 0.0) * fold(grad[0, 0])

    @pl.when(me < n - 1)
    def _():
        halo_k.wait_recv()
        for c in range(blocks):
            for copy in halo_pa(c):
                copy.wait_recv()
            here = pl.ds(c * ROWS, ROWS)
            prod = jnp.zeros((ROWS, width), jnp.float32)
            for t in range(steps):
                prod += (a[t, last, here] - halo_a[t, here]) * (p[t, last, here] - halo_p[t, here])
            k0, g_up = k[0, last, here], halo_g[here]
            factor = multiplier(code[0, last, here]) * act[last, here].astype(jnp.float32)
            w = weight(prod, factor, k0, g_up)
            w_up = w * k0
            ret_out[here] = w_up
            grad[0, last, here] = grad[0, last, here] + w * g_up
            if c < blocks - 1:
                returned(c).start()
            else:
                halo_first.wait_recv()
                acc[...] = acc[...] + fold(halo_own[...] + w_up)

    def take_back(c):
        here = pl.ds(c * ROWS, ROWS)
        returned(c).wait_recv()
        log0 = grad[0, 0, here] + ret_in[here]
        grad[0, 0, here] = log0
        return fold(log0)

    @pl.when(me > 0)
    def _():
        halo_first.wait_send()
        for c in range(blocks - 1):
            acc[...] = acc[...] + take_back(c)

    mine = jnp.sum(acc[...] + fold(grad[0, last]), axis=0, keepdims=True)
    part[...] = mine

    def to_peer(j):
        return pltpu.make_async_remote_copy(
            src_ref=part, dst_ref=parts.at[j - 1], send_sem=part_send.at[j - 1], recv_sem=part_recv.at[j - 1],
            device_id={"gx": lax.rem(me + j, n)}, device_id_type=MESH)

    def send(j, carry):
        to_peer(j).start()
        return carry

    def receive(j, carry):
        to_peer(j).wait_recv()
        return carry

    lax.fori_loop(1, n, send, 0)

    @pl.when(me < n - 1)
    def _():
        returned(blocks - 1).start()

    @pl.when(me > 0)
    def _():
        take_back(blocks - 1)

    lax.fori_loop(1, n, receive, 0)
    whole = jnp.sum(jnp.sum(parts[...], axis=0) + mine, keepdims=True)
    scale = jnp.broadcast_to(lax.rsqrt(whole / entries + epsilon), (ROWS, width))

    def normalize(i, carry):
        here = pl.ds(pl.multiple_of(i * ROWS, ROWS), ROWS)
        for d in range(3):
            for l in range(layers):
                grad[d, l, here] = grad[d, l, here] * scale
        return carry

    lax.fori_loop(0, blocks, normalize, 0)

    def drain(j, carry):
        to_peer(j).wait_send()
        return carry

    lax.fori_loop(1, n, drain, 0)

    @pl.when(me > 0)
    def _():
        halo_k.wait_send()
        for c in range(blocks):
            for copy in halo_pa(c):
                copy.wait_send()

    @pl.when(me < n - 1)
    def _():
        for c in range(blocks):
            returned(c).wait_send()


def local(pressure, adjoint, permeability, active, fault_codes):
    n = lax.axis_size("gx")
    steps, layers, height, width = pressure.shape
    blocks = height // ROWS
    entries = 3 * layers * n * height * width
    f32 = jnp.float32
    padded = height + PAD
    dma = pltpu.SemaphoreType.DMA
    return pl.pallas_call(
        functools.partial(kernel, n, entries),
        out_shape=pltpu.VMEM((3, layers, height, width), f32),
        in_specs=[pl.BlockSpec(memory_space=pltpu.HBM)] * 5,
        out_specs=pl.BlockSpec(memory_space=pltpu.VMEM),
        scratch_shapes=[
            pltpu.VMEM((steps, layers, padded, width), f32),
            pltpu.VMEM((steps, layers, padded, width), f32),
            pltpu.VMEM((3, layers, padded, width), f32),
            pltpu.VMEM((layers, padded, width), jnp.int32),
            pltpu.VMEM((3, layers, height, width), jnp.int32),
            pltpu.VMEM((steps, height, width), f32),
            pltpu.VMEM((steps, height, width), f32),
            pltpu.VMEM((height, width), f32),
            pltpu.VMEM((ROWS, width), f32),
            pltpu.VMEM((height, width), f32),
            pltpu.VMEM((height, width), f32),
            pltpu.VMEM((height, width), f32),
            pltpu.VMEM((padded, width), f32),
            pltpu.VMEM((8, width), f32),
            pltpu.VMEM((1, width), f32),
            pltpu.VMEM((n - 1, 1, width), f32),
            dma((5, layers)),
            dma((2 * blocks + 2,)),
            dma((2 * blocks + 2,)),
            dma((blocks,)),
            dma((blocks,)),
            dma((n - 1,)),
            dma((n - 1,)),
            pltpu.SemaphoreType.REGULAR((len(distances(n)) + 1,)),
        ],
        compiler_params=pltpu.CompilerParams(collective_id=0, has_side_effects=True, vmem_limit_bytes=GRANT),
        cost_estimate=pl.CostEstimate(flops=100_000_000, bytes_accessed=12_000_000, transcendentals=0),
    )(pressure, adjoint, permeability, active, fault_codes)


def solution(mesh):
    split = ("groups", "gx")
    placed = (P(None, split), P(None, split), P(None, split), P(split), P(None, split))
    return jax.shard_map(local, mesh=mesh, in_specs=placed, out_specs=P(None, split), check_vma=False)
```

profile of v0, /device:TPU:0, one launch (start us, length us, event | category | flops | bytes accessed | tf_op | source)
XLA Modules:
  0.0 24.4 jit_solution(8520292069927473896)
XLA Ops:
  0.0 23.3 %shard_map.55 = f32[3,8,128,128]{3,2,1,0:T(8,128)S(1)} custom-call(f32[7,8,128,128]{3,2,1,0:T(8,128)} %p_hbm.1, f32[7,8,128,128]{3,2,1,0:T(8,128)} %a_hbm.1, f32[3,8,128,128]{3,2,1,0:T(8,128)} %k_hbm.1, s32[8,128,128]{2,1,0:T(8,128)} %act_hbm.1, s32[3,8,128,128]{3,2,1,0:T(8,128)} %code_hbm.1), custom_call_target="tpu_custom_call" | custom-call | flops 100000000 | bytes 12000000 | tf_op jit(solution)/shard_map/pallas_call | solution.py:326
  23.3 1.1 %copy.7 = f32[3,8,128,128]{3,2,1,0:T(8,128)} copy(f32[3,8,128,128]{3,2,1,0:T(8,128)S(1)} %shard_map.55) | data formatting | bytes 3145728
where the time goes:
time: 24.6 us; the launch traced here: 24.4 us
  Pallas kernels  23.3 us (95%)
  local copies, waits for them, and re-layouts  1.15 us (5%)
    pallas_call x1, Pallas kernels, local(): pl.pallas_call(functools.partial(kernel, n, entries), out_shape=pltpu.VME...  23.3 us
    unnamed x1, local copies, waits for them, and re-layouts  1.15 us

commit v1 on v0

v1 whole, which is shorter than its diff:
```python
import functools

import jax
import jax.numpy as jnp
from jax import lax
from jax.experimental import pallas as pl
from jax.experimental.pallas import tpu as pltpu
from jax.sharding import PartitionSpec as P

MESH = pl.DeviceIdType.MESH
epsilon = 1e-06
ROWS = 64
CHUNK = 8
LATE = 4
PAD = 8
GRANT = 58_000_000


def doubled(codes):
    return jnp.where(codes == 0, 2.0, jnp.where(codes == 1, 1.2, jnp.where(codes == 2, 0.5, 0.1))).astype(jnp.float32)


def fold(values):
    squares = values * values
    total = squares[0:8]
    for i in range(8, squares.shape[0], 8):
        total = total + squares[i : i + 8]
    return total


def weight(products, factor, k_lo, k_up):
    summed = k_lo + k_up
    return factor * products * (k_lo * k_up) / jnp.maximum(summed * summed, 1e-30)


def distances(n):
    reach, rounds = 1, []
    while reach < n - 1:
        rounds.append(reach)
        reach *= 2
    return rounds


def down_shares(chips, chunks):
    return [max(chunks - (3 * chunks * q * q) // (4 * max(chips - 2, 1) ** 2), 0) for q in range(chips - 1)]


def kernel(
    n, p_hbm, a_hbm, k_hbm, act_hbm, code_hbm, grad, scale_out,
    pa, k, act, code, halo_t, halo_b, ret_t_out, ret_b_out, ret_t_in, ret_b_in, tail, part, parts,
    load_sem, chunk_recv, sems, near_sem,
):
    me = lax.axis_index("gx")
    lower, upper = me - 1, me + 1
    steps, layers, height, width = p_hbm.shape
    last = layers - 1
    blocks = height // ROWS
    chunks = height // CHUNK
    entries = 3 * layers * n * height * width
    K, FACTOR = 2 * steps, 2 * steps + 1
    OWN_UP, OWN_LO = 2 * steps + 1, 2 * steps + 2
    SEND, SEND_LATE, BACK_SEND, BACK, BACK_LATE, PAIR_SEND, PAIR, PAIR_BACK, PART_SEND, PART = range(10)

    odd = me % 2
    even = odd == 0
    odd = odd == 1
    has_lo, has_up = me > 0, me < n - 1
    apart = jnp.where(even, me, n - 1 - me) > 0
    chip = (me + 1) // 2 - 1
    shares = down_shares(n // 2, chunks)
    share = jnp.int32(0)
    for q, value in enumerate(shares):
        share = jnp.where(chip == q, value, share)
    share = jnp.where(apart, share, 0)
    rows_end = jnp.where(apart, chunks, 0)
    late_down = jnp.where(share > LATE, share - LATE, 0)
    late_up = jnp.where(rows_end - LATE > share, rows_end - LATE, share)

    def loop(start, stop, body):
        def step(i, carry):
            body(i)
            return carry

        lax.fori_loop(start, stop, step, 0)

    barrier = pltpu.get_barrier_semaphore()

    def signal(semaphore, distance):
        for there, inside in ((me - distance, me >= distance), (me + distance, me + distance < n)):
            @pl.when(inside)
            def _():
                pl.semaphore_signal(semaphore, inc=1, device_id={"gx": there}, device_id_type=MESH)

    def await_signals(semaphore, distance):
        peers = jnp.where(me >= distance, 1, 0) + jnp.where(me + distance < n, 1, 0)
        pl.semaphore_wait(semaphore, peers)

    signal(barrier, 1)
    rounds = distances(n)

    def turn(i):
        if i > 0:
            await_signals(near_sem.at[i - 1], rounds[i - 1])
        if i < len(rounds):
            signal(near_sem.at[i], rounds[i])

    def fields(l, sem):
        return (
            pltpu.make_async_copy(p_hbm.at[:, l], pa.at[pl.ds(0, steps), l, pl.ds(0, height)], sem),
            pltpu.make_async_copy(a_hbm.at[:, l], pa.at[pl.ds(steps, steps), l, pl.ds(0, height)], sem),
        )

    def cells(l, sem):
        return (
            pltpu.make_async_copy(k_hbm.at[:, l], k.at[:, l, pl.ds(0, height)], sem),
            pltpu.make_async_copy(act_hbm.at[l], act.at[l, pl.ds(0, height)], sem),
            pltpu.make_async_copy(code_hbm.at[:, l], code.at[:, l], sem),
        )

    def start_layer(l, sem):
        for copy in fields(l, sem) + cells(l, sem):
            copy.start()

    def await_planes(planes, rank, sem):
        ref = pa.at[pl.ds(0, planes), pl.ds(0, rank), pl.ds(0, height)]
        pltpu.make_async_copy(ref, ref, sem).wait()

    def layer_sem(l):
        return load_sem.at[l + 1]


    def chunk_rows(c):
        return pl.ds(pl.multiple_of(c * CHUNK, CHUNK), CHUNK)

    def down(c, planes, kind):
        rows = chunk_rows(c)
        return pltpu.make_async_remote_copy(
            src_ref=pa.at[pl.ds(0, planes), 0, rows], dst_ref=halo_t.at[pl.ds(0, planes), rows],
            send_sem=sems.at[kind], recv_sem=chunk_recv.at[c], device_id={"gx": lower}, device_id_type=MESH)

    def up(c, planes, kind):
        rows = chunk_rows(c)
        return pltpu.make_async_remote_copy(
            src_ref=pa.at[pl.ds(0, planes), last, rows], dst_ref=halo_b.at[pl.ds(0, planes), rows],
            send_sem=sems.at[kind], recv_sem=chunk_recv.at[c], device_id={"gx": upper}, device_id_type=MESH)

    def back_up(c, kind):
        rows = chunk_rows(c)
        return pltpu.make_async_remote_copy(
            src_ref=ret_t_out.at[rows], dst_ref=ret_b_in.at[rows],
            send_sem=sems.at[BACK_SEND], recv_sem=sems.at[kind], device_id={"gx": upper}, device_id_type=MESH)

    def back_down(c, kind):
        rows = chunk_rows(c)
        return pltpu.make_async_remote_copy(
            src_ref=ret_b_out.at[rows], dst_ref=ret_t_in.at[rows],
            send_sem=sems.at[BACK_SEND], recv_sem=sems.at[kind], device_id={"gx": lower}, device_id_type=MESH)

    D, DL, U, UL = 2 * steps + 1, 2 * steps + 2, 2 * steps + 2, 2 * steps + 3

    pair = pltpu.make_async_remote_copy(
        src_ref=pa.at[pl.ds(0, D), 0, pl.ds(0, height)], dst_ref=halo_t.at[pl.ds(0, D)],
        send_sem=sems.at[PAIR_SEND], recv_sem=sems.at[PAIR], device_id={"gx": lower}, device_id_type=MESH)
    pair_back = pltpu.make_async_remote_copy(
        src_ref=ret_t_out, dst_ref=ret_b_in,
        send_sem=sems.at[PAIR_SEND], recv_sem=sems.at[PAIR_BACK], device_id={"gx": upper}, device_id_type=MESH)

    def await_bytes(ref, sem):
        pltpu.make_async_copy(ref, ref, sems.at[sem]).wait()

    def await_rows(ref, count, sem):
        if count > 0:
            await_bytes(ref.at[pl.ds(0, count * CHUNK)], sem)

    def await_planes_of(ref, planes, count, sem):
        if count > 0:
            await_bytes(ref.at[pl.ds(0, planes), pl.ds(0, count * CHUNK)], sem)

    def each_share(side, body):
        for value in sorted(set(shares)):
            @pl.when(jnp.logical_and(jnp.logical_and(apart, side), share == value))
            def _(value=value):
                body(value, max(value - LATE, 0), max(chunks - LATE, value))

    for l in (0, last):
        for copy in fields(l, load_sem.at[0]):
            copy.start()
    pltpu.make_async_copy(k_hbm.at[0, last], pa.at[K, last, pl.ds(0, height)], load_sem.at[1]).start()
    for l in (0, last):
        for copy in cells(l, load_sem.at[1]):
            copy.start()

    tail[0:8] = jnp.zeros((8, width), jnp.float32)

    def clear(l):
        for t in range(2 * steps):
            pa[t, l, height:] = jnp.zeros((PAD, width), jnp.float32)
        k[1, l, height:] = jnp.zeros((PAD, width), jnp.float32)
        act[l, height:] = jnp.zeros((PAD, width), jnp.int32)

    loop(0, layers, clear)

    await_planes(2 * 7 + 1, 1, load_sem.at[1])
    pa[K, 0, 0:height] = k[0, 0, 0:height] * act[0, 0:height].astype(jnp.float32)
    pa[FACTOR, last, 0:height] = doubled(code[0, last]) * act[last, 0:height].astype(jnp.float32)
    await_planes(2 * steps, 2, load_sem.at[0])
    await_signals(barrier, 1)

    @pl.when(even)
    def _():
        loop(0, late_down, lambda c: down(c, D, SEND).start())

    @pl.when(odd)
    def _():
        loop(share, late_up, lambda c: up(c, U, SEND).start())
        pair.start()

    start_layer(1, load_sem.at[2])
    start_layer(last - 1, load_sem.at[2])
    loop(2, last - 1, lambda l: start_layer(l, layer_sem(l)))
    turn(0)

    zero = jnp.zeros((ROWS, width), jnp.float32)
    lane = lax.broadcasted_iota(jnp.int32, (ROWS, width), 1)
    for l in range(2, last - 1):
        grad[0, l] = jnp.zeros((height, width), jnp.float32)

    def opened(l, rows):
        return act[l, rows].astype(jnp.float32)

    def cross(l):
        def block(b):
            here = pl.ds(pl.multiple_of(b * ROWS, ROWS), ROWS)
            prod = zero
            for t in range(steps):
                prod += (pa[steps + t, l, here] - pa[steps + t, l + 1, here]) * (pa[t, l, here] - pa[t, l + 1, here])
            k0, k0_up = k[0, l, here] * opened(l, here), k[0, l + 1, here] * opened(l + 1, here)
            w = weight(prod, doubled(code[0, l, here]), k0, k0_up)
            grad[0, l, here] = w * k0_up
            grad[0, l + 1, here] = w * k0

        loop(0, blocks, block)

    await_planes(2 * steps, 3, load_sem.at[2])
    cross(0)
    cross(last - 1)
    pa[OWN_UP, 0, 0:height] = grad[0, 0]
    pa[OWN_LO, last, 0:height] = grad[0, last]

    @pl.when(even)
    def _():
        loop(late_down, share, lambda c: down(c, DL, SEND_LATE).start())

    @pl.when(odd)
    def _():
        loop(late_up, rows_end, lambda c: up(c, UL, SEND_LATE).start())

    def lanes_weight(l, r, prod):
        here = pl.ds(r, ROWS)
        k2 = k[2, l, here] * opened(l, here)
        k2_up = jnp.where(lane < width - 1, pltpu.roll(k2, width - 1, 1), 0.0)
        w = weight(prod, doubled(code[2, l, here]), k2, k2_up)
        return w * k2_up, w * k2

    def lanes_store(l, r, w_lo, w_up):
        log2 = w_lo + pltpu.roll(w_up, 1, 1)
        grad[2, l, pl.ds(r, ROWS)] = log2
        return fold(log2)

    def layer(l, carry, crossing):
        def block(b, carry):
            total, prod_z, w_lo, w_up, l1, r1, l2, r2 = carry
            r = pl.multiple_of(b * ROWS, ROWS)
            here, after = pl.ds(r, ROWS), pl.ds(r + 1, ROWS)
            total = total + lanes_store(l2, pl.multiple_of(r2, ROWS), w_lo, w_up)
            w_lo, w_up = lanes_weight(l1, pl.multiple_of(r1, ROWS), prod_z)
            prod_x, prod_y, prod_z = zero, zero, zero
            for t in range(steps):
                pt, at = pa[t, l, here], pa[steps + t, l, here]
                prod_z += (at - pltpu.roll(at, width - 1, 1)) * (pt - pltpu.roll(pt, width - 1, 1))
                prod_y += (at - pa[steps + t, l, after]) * (pt - pa[t, l, after])
                if crossing:
                    prod_x += (at - pa[steps + t, l + 1, here]) * (pt - pa[t, l + 1, here])
            now = opened(l, here)
            k1, k1_up = k[1, l, here] * now, k[1, l, after] * opened(l, after)
            w = weight(prod_y, doubled(code[1, l, here]), k1, k1_up)
            tail[pl.ds(r + 8, ROWS)] = w * k1
            log1 = w * k1_up + tail[pl.ds(r + 7, ROWS)]
            grad[1, l, here] = log1
            total = total + fold(log1)
            if crossing:
                k0, k0_up = k[0, l, here] * now, k[0, l + 1, here] * opened(l + 1, here)
                w = weight(prod_x, doubled(code[0, l, here]), k0, k0_up)
                log0 = grad[0, l, here] + w * k0_up
                grad[0, l, here] = log0
                grad[0, l + 1, here] = grad[0, l + 1, here] + w * k0
                total = total + fold(log0)
            return total, prod_z, w_lo, w_up, l, r, l1, r1

        return lax.fori_loop(0, blocks, block, carry)

    def border(i, carry):
        return layer(jnp.where(i == 0, 0, last + 1 - i), carry, False)

    def inner(l, carry):
        @pl.when(l < last - 2)
        def _():
            await_planes(steps, 3, layer_sem(l + 1))

        @pl.when(l == 2)
        def _():
            turn(1)

        return layer(l, carry, True)

    nothing = (jnp.zeros((8, width), jnp.float32), zero, zero, zero) + (jnp.int32(0),) * 4
    carry = lax.fori_loop(0, 3, border, nothing)
    total, prod_z, w_lo, w_up, l1, r1, l2, r2 = lax.fori_loop(1, last - 1, inner, carry)
    total = total + lanes_store(l2, pl.multiple_of(r2, ROWS), w_lo, w_up)
    w_lo, w_up = lanes_weight(l1, pl.multiple_of(r1, ROWS), prod_z)
    total = total + lanes_store(l1, pl.multiple_of(r1, ROWS), w_lo, w_up)
    total = total + fold(grad[0, last - 1])
    total = total + jnp.where(has_lo, 0.0, 1.0) * fold(grad[0, 0]) + jnp.where(has_up, 0.0, 1.0) * fold(grad[0, last])
    turn(2)

    def square(values):
        return values * values

    def face_top(rows, size):
        prod = jnp.zeros((size, width), jnp.float32)
        for t in range(steps):
            prod += (pa[steps + t, last, rows] - halo_t[steps + t, rows]) * (pa[t, last, rows] - halo_t[t, rows])
        k0, g_up = k[0, last, rows], halo_t[K, rows]
        w = weight(prod, pa[FACTOR, last, rows], k0, g_up)
        w_up = w * k0
        ret_t_out[rows] = w_up
        log0 = grad[0, last, rows] + w * g_up
        grad[0, last, rows] = log0
        return fold(log0), w_up

    def face_bottom(rows, size):
        prod = jnp.zeros((size, width), jnp.float32)
        for t in range(steps):
            prod += (halo_b[steps + t, rows] - pa[steps + t, 0, rows]) * (halo_b[t, rows] - pa[t, 0, rows])
        k0, g_up = halo_b[K, rows], pa[K, 0, rows]
        w = weight(prod, halo_b[FACTOR, rows], k0, g_up)
        w_lo = w * g_up
        ret_b_out[rows] = w_lo
        log0 = grad[0, 0, rows] + w * k0
        grad[0, 0, rows] = log0
        return fold(log0), w_lo

    def pair_face(b, total):
        squares, _ = face_top(pl.ds(pl.multiple_of(b * 32, 32), 32), 32)
        return total + squares

    @pl.when(even)
    def _():
        pair.wait_recv()

    total = lax.fori_loop(0, jnp.where(even, height // 32, 0), pair_face, total)

    @pl.when(even)
    def _():
        pair_back.start()

    def top_early(c, total):
        down(c, D, SEND).wait_recv()
        squares, _ = face_top(chunk_rows(c), CHUNK)
        back_up(c, BACK).start()
        return total + squares

    def top_late(c, total):
        down(c, DL, SEND_LATE).wait_recv()
        squares, w_up = face_top(chunk_rows(c), CHUNK)
        back_up(c, BACK_LATE).start()
        return total + squares + fold(halo_t[OWN_UP, chunk_rows(c)] + w_up)

    def bottom_early(c, total):
        up(c, U, SEND).wait_recv()
        squares, _ = face_bottom(chunk_rows(c), CHUNK)
        back_down(c, BACK).start()
        return total + squares

    def bottom_late(c, total):
        up(c, UL, SEND_LATE).wait_recv()
        squares, w_lo = face_bottom(chunk_rows(c), CHUNK)
        back_down(c, BACK_LATE).start()
        return total + squares + fold(halo_b[OWN_LO, chunk_rows(c)] + w_lo)

    def add_bottom(c, total):
        rows = chunk_rows(c)
        log0 = grad[0, 0, rows] + ret_b_in[rows]
        grad[0, 0, rows] = log0
        return total + fold(log0)

    def add_top(c, total):
        rows = chunk_rows(c)
        log0 = grad[0, last, rows] + ret_t_in[rows]
        grad[0, last, rows] = log0
        return total + fold(log0)

    def when_even(value):
        return jnp.where(even, value, 0)

    def when_odd(value):
        return jnp.where(odd, value, 0)

    @pl.when(odd)
    def _():
        pair_back.wait_recv()

    total = lax.fori_loop(0, when_odd(chunks), add_bottom, total)
    total = lax.fori_loop(0, when_odd(late_down), top_early, total)
    total = lax.fori_loop(when_even(share), when_even(late_up), bottom_early, total)
    for i in range(3, len(rounds)):
        turn(i)
    total = lax.fori_loop(when_odd(late_down), when_odd(share), top_late, total)
    total = lax.fori_loop(when_even(late_up), when_even(rows_end), bottom_late, total)
    each_share(even, lambda value, below, above: await_rows(ret_b_in, below, BACK))
    each_share(odd, lambda value, below, above: await_rows(ret_t_in, above - value, BACK))
    total = lax.fori_loop(0, when_even(late_down), add_bottom, total)
    total = lax.fori_loop(when_odd(share), when_odd(late_up), add_top, total)

    turn(len(rounds))
    mine = jnp.sum(total, axis=0, keepdims=True)
    part[...] = mine

    def to_peer(j):
        return pltpu.make_async_remote_copy(
            src_ref=part, dst_ref=parts.at[me], send_sem=sems.at[PART_SEND], recv_sem=sems.at[PART],
            device_id={"gx": j}, device_id_type=MESH)

    loop(0, me, lambda j: to_peer(j).start())
    loop(me + 1, n, lambda j: to_peer(j).start())
    parts[me] = mine

    each_share(even, lambda value, below, above: await_rows(ret_b_in, value - below, BACK_LATE))
    each_share(odd, lambda value, below, above: await_rows(ret_t_in, chunks - above, BACK_LATE))
    nowhere = jnp.zeros((8, width), jnp.float32)
    lax.fori_loop(when_even(late_down), when_even(share), add_bottom, nowhere)
    lax.fori_loop(when_odd(late_up), when_odd(rows_end), add_top, nowhere)

    def drain_even(value, below, above):
        await_planes_of(halo_t, D, below, SEND)
        await_planes_of(halo_t, DL, value - below, SEND_LATE)
        await_rows(ret_b_out, chunks - value, BACK_SEND)

    def drain_odd(value, below, above):
        await_planes_of(halo_b, U, above - value, SEND)
        await_planes_of(halo_b, UL, chunks - above, SEND_LATE)
        await_rows(ret_t_out, value, BACK_SEND)

    each_share(even, drain_even)
    each_share(odd, drain_odd)

    @pl.when(even)
    def _():
        pair_back.wait_send()

    @pl.when(odd)
    def _():
        pair.wait_send()

    others = parts.at[pl.ds(0, n - 1)]
    pltpu.make_async_copy(others, others, sems.at[PART_SEND]).wait()
    pltpu.make_async_copy(others, others, sems.at[PART]).wait()
    whole = jnp.sum(jnp.sum(parts[...], axis=0), keepdims=True)
    scale_out[...] = jnp.broadcast_to(lax.rsqrt(whole / entries + epsilon), scale_out.shape)


def finish(raw, scale, out, scaled, sem):
    dims, layers = raw.shape[:2]
    factor = jnp.broadcast_to(scale[0:1], raw.shape[2:])
    copies = []
    for l in range(layers):
        for d in range(dims):
            scaled[d, l] = raw[d, l] * factor
        copies.append(pltpu.make_async_copy(scaled.at[:, l], out.at[:, l], sem.at[l]))
        copies[-1].start()
    for copy in copies:
        copy.wait()


def local(pressure, adjoint, permeability, active, fault_codes):
    n = lax.axis_size("gx")
    steps, layers, height, width = pressure.shape
    chunks = height // CHUNK
    f32 = jnp.float32
    padded = height + PAD
    dma = pltpu.SemaphoreType.DMA
    raw, scale = pl.pallas_call(
        functools.partial(kernel, n),
        out_shape=(pltpu.VMEM((3, layers, height, width), f32), pltpu.VMEM((8, width), f32)),
        in_specs=[pl.BlockSpec(memory_space=pltpu.HBM)] * 5,
        out_specs=(pl.BlockSpec(memory_space=pltpu.VMEM), pl.BlockSpec(memory_space=pltpu.VMEM)),
        scratch_shapes=[
            pltpu.VMEM((2 * steps + 3, layers, padded, width), f32),
            pltpu.VMEM((3, layers, padded, width), f32),
            pltpu.VMEM((layers, padded, width), jnp.int32),
            pltpu.VMEM((3, layers, height, width), jnp.int32),
            pltpu.VMEM((2 * steps + 2, height, width), f32),
            pltpu.VMEM((2 * steps + 3, height, width), f32),
            pltpu.VMEM((height, width), f32),
            pltpu.VMEM((height, width), f32),
            pltpu.VMEM((height, width), f32),
            pltpu.VMEM((height, width), f32),
            pltpu.VMEM((padded, width), f32),
            pltpu.VMEM((1, width), f32),
            pltpu.VMEM((n, 1, width), f32),
            dma((layers - 1,)),
            dma((chunks,)),
            dma((10,)),
            pltpu.SemaphoreType.REGULAR((len(distances(n)),)),
        ],
        compiler_params=pltpu.CompilerParams(collective_id=0, has_side_effects=True, vmem_limit_bytes=GRANT),
        cost_estimate=pl.CostEstimate(flops=100_000_000, bytes_accessed=12_000_000, transcendentals=0),
        name="faces",
    )(pressure, adjoint, permeability, active, fault_codes)
    return pl.pallas_call(
        finish,
        out_shape=jax.ShapeDtypeStruct(raw.shape, f32),
        in_specs=[pl.BlockSpec(memory_space=pltpu.VMEM)] * 2,
        out_specs=pl.BlockSpec(memory_space=pltpu.HBM),
        scratch_shapes=[pltpu.VMEM((3, layers, height, width), f32), dma((layers,))],
        compiler_params=pltpu.CompilerParams(vmem_limit_bytes=8_000_000),
        name="finish",
    )(raw, scale)


def solution(mesh):
    split = ("groups", "gx")
    placed = (P(None, split), P(None, split), P(None, split), P(split), P(None, split))
    return jax.shard_map(local, mesh=mesh, in_specs=placed, out_specs=P(None, split), check_vma=False)
```

time: 24.6 us -> 22.5 us (0.915)
  local copies, waits for them, and re-layouts: 1.15 us -> 0 us
  Pallas kernels: 23.3 us -> 22.4 us
    unnamed x1 -> x0, local copies, waits for them, and re-layouts: 1.15 us -> none
    pallas_call x1 -> x2, Pallas kernels: 23.3 us -> 22.4 us  [the longest x1 21.2 us: local(): pl.pallas_call(functools.partial(kernel, n), out_shape=(pltpu.VMEM((3, la...]
where the time goes in v1:
time: 22.5 us; the launch traced here: 22.4 us
  Pallas kernels  22.4 us (100%)
    pallas_call x1, Pallas kernels, local(): pl.pallas_call(functools.partial(kernel, n), out_shape=(pltpu.VMEM((3, la...  21.2 us
    pallas_call x1, Pallas kernels, local(): pl.pallas_call(finish, out_shape=jax.ShapeDtypeStruct(raw.shape, f32), in...  1.21 us

profile of v1, /device:TPU:0, one launch (start us, length us, event | category | flops | bytes accessed | tf_op | source)
XLA Modules:
  0.0 22.4 jit_solution(18435200240739128469)
XLA Ops:
  0.0 21.2 %faces.1 = (f32[3,8,128,128]{3,2,1,0:T(8,128)S(1)}, f32[8,128]{1,0:T(8,128)S(1)}) custom-call(f32[7,8,128,128]{3,2,1,0:T(8,128)} %p_hbm.1, f32[7,8,128,128]{3,2,1,0:T(8,128)} %a_hbm.1, f32[3,8,128,128]{3,2,1,0:T(8,128)} %k_hbm.1, s32[8,128,128]{2,1,0:T(8,128)} %act_hbm.1, s32[3,8,128,128]{3,2,1,0:T(8,128)} %code_hbm.1), custom_call_target="tpu_custom_call" | custom-call | flops 100000000 | bytes 12000000 | tf_op jit(solution)/shard_map/faces/pallas_call | solution.py:492
  21.2 1.2 %finish.1 = f32[3,8,128,128]{3,2,1,0:T(8,128)} custom-call(f32[3,8,128,128]{3,2,1,0:T(8,128)S(1)} %get-tuple-element.7.raw, f32[8,128]{1,0:T(8,128)S(1)} %get-tuple-element.8.scale), custom_call_target="tpu_custom_call" | custom-call | tf_op jit(solution)/shard_map/finish/pallas_call | solution.py:520

commit v2 on v1

--- a/solution.py
+++ b/solution.py
@@ -12,6 +12,7 @@
 ROWS = 64
 CHUNK = 8
 LATE = 4
+HEAD = 2
 PAD = 8
 GRANT = 58_000_000
 
@@ -99,34 +100,42 @@
     rounds = distances(n)
 
     def turn(i):
-        if i > 0:
+        if 0 < i <= len(rounds):
             await_signals(near_sem.at[i - 1], rounds[i - 1])
         if i < len(rounds):
             signal(near_sem.at[i], rounds[i])
 
-    def fields(l, sem):
+    def fields(l, sem, start=0, stop=height):
+        rows = pl.ds(start, stop - start)
         return (
-            pltpu.make_async_copy(p_hbm.at[:, l], pa.at[pl.ds(0, steps), l, pl.ds(0, height)], sem),
-            pltpu.make_async_copy(a_hbm.at[:, l], pa.at[pl.ds(steps, steps), l, pl.ds(0, height)], sem),
+            pltpu.make_async_copy(p_hbm.at[:, l, rows], pa.at[pl.ds(0, steps), l, rows], sem),
+            pltpu.make_async_copy(a_hbm.at[:, l, rows], pa.at[pl.ds(steps, steps), l, rows], sem),
         )
 
+    def k_of(start, stop, l, sem):
+        axes = pl.ds(start, stop - start)
+        return pltpu.make_async_copy(k_hbm.at[axes, l], k.at[axes, l, pl.ds(0, height)], sem)
+
+    def code_of(start, stop, l, sem):
+        axes = pl.ds(start, stop - start)
+        return pltpu.make_async_copy(code_hbm.at[axes, l], code.at[axes, l], sem)
+
+    def act_of(l, sem):
+        return pltpu.make_async_copy(act_hbm.at[l], act.at[l, pl.ds(0, height)], sem)
+
     def cells(l, sem):
-        return (
-            pltpu.make_async_copy(k_hbm.at[:, l], k.at[:, l, pl.ds(0, height)], sem),
-            pltpu.make_async_copy(act_hbm.at[l], act.at[l, pl.ds(0, height)], sem),
-            pltpu.make_async_copy(code_hbm.at[:, l], code.at[:, l], sem),
-        )
+        return k_of(0, 3, l, sem), act_of(l, sem), code_of(0, 3, l, sem)
 
     def start_layer(l, sem):
         for copy in fields(l, sem) + cells(l, sem):
             copy.start()
 
-    def await_planes(planes, rank, sem):
-        ref = pa.at[pl.ds(0, planes), pl.ds(0, rank), pl.ds(0, height)]
+    def await_planes(planes, rank, sem, rows=height):
+        ref = pa.at[pl.ds(0, planes), pl.ds(0, rank), pl.ds(0, rows)]
         pltpu.make_async_copy(ref, ref, sem).wait()
 
     def layer_sem(l):
-        return load_sem.at[l + 1]
+        return load_sem.at[l + 2]
 
 
     def chunk_rows(c):
@@ -182,13 +191,14 @@
             def _(value=value):
                 body(value, max(value - LATE, 0), max(chunks - LATE, value))
 
-    for l in (0, last):
-        for copy in fields(l, load_sem.at[0]):
-            copy.start()
-    pltpu.make_async_copy(k_hbm.at[0, last], pa.at[K, last, pl.ds(0, height)], load_sem.at[1]).start()
-    for l in (0, last):
-        for copy in cells(l, load_sem.at[1]):
-            copy.start()
+    head = HEAD * CHUNK
+    load_k = pltpu.make_async_copy(k_hbm.at[0, last], pa.at[K, last, pl.ds(0, height)], load_sem.at[2])
+    for copy in (
+        (k_of(0, 1, 0, load_sem.at[0]), act_of(0, load_sem.at[0])) + fields(0, load_sem.at[0], 0, head)
+        + fields(0, load_sem.at[1], head)
+        + (load_k, act_of(last, load_sem.at[2]), code_of(0, 1, last, load_sem.at[2])) + fields(last, load_sem.at[2])
+    ):
+        copy.start()
 
     tail[0:8] = jnp.zeros((8, width), jnp.float32)
 
@@ -200,23 +210,36 @@
 
     loop(0, layers, clear)
 
-    await_planes(2 * 7 + 1, 1, load_sem.at[1])
+    await_signals(barrier, 1)
+    await_planes(8, 1, load_sem.at[0], (2 * steps * head + 2 * height) // 8)
     pa[K, 0, 0:height] = k[0, 0, 0:height] * act[0, 0:height].astype(jnp.float32)
+    ahead = jnp.where(late_down < HEAD, late_down, HEAD)
+
+    @pl.when(even)
+    def _():
+        loop(0, ahead, lambda c: down(c, D, SEND).start())
+
+    await_planes(2 * steps, 1, load_sem.at[1], height - head)
+
+    @pl.when(even)
+    def _():
+        loop(ahead, late_down, lambda c: down(c, D, SEND).start())
+
+    await_planes(2 * steps + 3, 1, load_sem.at[2])
     pa[FACTOR, last, 0:height] = doubled(code[0, last]) * act[last, 0:height].astype(jnp.float32)
-    await_planes(2 * steps, 2, load_sem.at[0])
-    await_signals(barrier, 1)
-
-    @pl.when(even)
-    def _():
-        loop(0, late_down, lambda c: down(c, D, SEND).start())
 
     @pl.when(odd)
     def _():
         loop(share, late_up, lambda c: up(c, U, SEND).start())
         pair.start()
 
-    start_layer(1, load_sem.at[2])
-    start_layer(last - 1, load_sem.at[2])
+    for copy in (
+        k_of(1, 3, 0, load_sem.at[3]), code_of(0, 3, 0, load_sem.at[3]),
+        k_of(0, 3, last, load_sem.at[3]), code_of(1, 3, last, load_sem.at[3]),
+    ):
+        copy.start()
+    start_layer(1, load_sem.at[3])
+    start_layer(last - 1, load_sem.at[3])
     loop(2, last - 1, lambda l: start_layer(l, layer_sem(l)))
     turn(0)
 
@@ -241,9 +264,10 @@
 
         loop(0, blocks, block)
 
-    await_planes(2 * steps, 3, load_sem.at[2])
+    await_planes(2 * steps - 1, 4, load_sem.at[3])
     cross(0)
     cross(last - 1)
+    turn(1)
     pa[OWN_UP, 0, 0:height] = grad[0, 0]
     pa[OWN_LO, last, 0:height] = grad[0, last]
 
@@ -307,9 +331,10 @@
         def _():
             await_planes(steps, 3, layer_sem(l + 1))
 
-        @pl.when(l == 2)
-        def _():
-            turn(1)
+        for i, at_layer in ((2, 1), (3, last - 3)):
+            @pl.when(l == at_layer)
+            def _(i=i):
+                turn(i)
 
         return layer(l, carry, True)
 
@@ -321,8 +346,6 @@
     total = total + lanes_store(l1, pl.multiple_of(r1, ROWS), w_lo, w_up)
     total = total + fold(grad[0, last - 1])
     total = total + jnp.where(has_lo, 0.0, 1.0) * fold(grad[0, 0]) + jnp.where(has_up, 0.0, 1.0) * fold(grad[0, last])
-    turn(2)
-
     def square(values):
         return values * values
 
@@ -413,16 +436,15 @@
     total = lax.fori_loop(0, when_odd(chunks), add_bottom, total)
     total = lax.fori_loop(0, when_odd(late_down), top_early, total)
     total = lax.fori_loop(when_even(share), when_even(late_up), bottom_early, total)
-    for i in range(3, len(rounds)):
+    for i in range(4, len(rounds) + 1):
         turn(i)
-    total = lax.fori_loop(when_odd(late_down), when_odd(share), top_late, total)
-    total = lax.fori_loop(when_even(late_up), when_even(rows_end), bottom_late, total)
     each_share(even, lambda value, below, above: await_rows(ret_b_in, below, BACK))
     each_share(odd, lambda value, below, above: await_rows(ret_t_in, above - value, BACK))
     total = lax.fori_loop(0, when_even(late_down), add_bottom, total)
     total = lax.fori_loop(when_odd(share), when_odd(late_up), add_top, total)
-
-    turn(len(rounds))
+    total = lax.fori_loop(when_odd(late_down), when_odd(share), top_late, total)
+    total = lax.fori_loop(when_even(late_up), when_even(rows_end), bottom_late, total)
+
     mine = jnp.sum(total, axis=0, keepdims=True)
     part[...] = mine
 
@@ -472,14 +494,11 @@
 def finish(raw, scale, out, scaled, sem):
     dims, layers = raw.shape[:2]
     factor = jnp.broadcast_to(scale[0:1], raw.shape[2:])
-    copies = []
-    for l in range(layers):
-        for d in range(dims):
+    for d in range(dims):
+        for l in range(layers):
             scaled[d, l] = raw[d, l] * factor
-        copies.append(pltpu.make_async_copy(scaled.at[:, l], out.at[:, l], sem.at[l]))
-        copies[-1].start()
-    for copy in copies:
-        copy.wait()
+            pltpu.make_async_copy(scaled.at[d, l], out.at[d, l], sem.at[0]).start()
+    pltpu.make_async_copy(scaled, out, sem.at[0]).wait()
 
 
 def local(pressure, adjoint, permeability, active, fault_codes):
@@ -508,7 +527,7 @@
             pltpu.VMEM((padded, width), f32),
             pltpu.VMEM((1, width), f32),
             pltpu.VMEM((n, 1, width), f32),
-            dma((layers - 1,)),
+            dma((layers,)),
             dma((chunks,)),
             dma((10,)),
             pltpu.SemaphoreType.REGULAR((len(distances(n)),)),
@@ -522,7 +541,7 @@
         out_shape=jax.ShapeDtypeStruct(raw.shape, f32),
         in_specs=[pl.BlockSpec(memory_space=pltpu.VMEM)] * 2,
         out_specs=pl.BlockSpec(memory_space=pltpu.HBM),
-        scratch_shapes=[pltpu.VMEM((3, layers, height, width), f32), dma((layers,))],
+        scratch_shapes=[pltpu.VMEM((3, layers, height, width), f32), dma((1,))],
         compiler_params=pltpu.CompilerParams(vmem_limit_bytes=8_000_000),
         name="finish",
     )(raw, scale)

time: 22.5 us -> 21.6 us (0.960)
  Pallas kernels: 22.4 us -> 21.5 us
    pallas_call x1, Pallas kernels: 21.2 us -> 20.4 us  [local(): pl.pallas_call(functools.partial(kernel, n), out_shape=(pltpu.VMEM((3, la...]
where the time goes in v2:
time: 21.6 us; the launch traced here: 21.5 us
  Pallas kernels  21.5 us (100%)
    pallas_call x1, Pallas kernels, local(): pl.pallas_call(functools.partial(kernel, n), out_shape=(pltpu.VMEM((3, la...  20.4 us
    pallas_call x1, Pallas kernels, local(): pl.pallas_call(finish, out_shape=jax.ShapeDtypeStruct(raw.shape, f32), in...  1.13 us

profile of v2, /device:TPU:0, one launch (start us, length us, event | category | flops | bytes accessed | tf_op | source)
XLA Modules:
  0.0 21.5 jit_solution(15632794082344100100)
XLA Ops:
  0.0 20.4 %faces.1 = (f32[3,8,128,128]{3,2,1,0:T(8,128)S(1)}, f32[8,128]{1,0:T(8,128)S(1)}) custom-call(f32[7,8,128,128]{3,2,1,0:T(8,128)} %p_hbm.1, f32[7,8,128,128]{3,2,1,0:T(8,128)} %a_hbm.1, f32[3,8,128,128]{3,2,1,0:T(8,128)} %k_hbm.1, s32[8,128,128]{2,1,0:T(8,128)} %act_hbm.1, s32[3,8,128,128]{3,2,1,0:T(8,128)} %code_hbm.1), custom_call_target="tpu_custom_call" | custom-call | flops 100000000 | bytes 12000000 | tf_op jit(solution)/shard_map/faces/pallas_call | solution.py:511
  20.4 1.1 %finish.1 = f32[3,8,128,128]{3,2,1,0:T(8,128)} custom-call(f32[3,8,128,128]{3,2,1,0:T(8,128)S(1)} %get-tuple-element.7.raw, f32[8,128]{1,0:T(8,128)S(1)} %get-tuple-element.8.scale), custom_call_target="tpu_custom_call" | custom-call | tf_op jit(solution)/shard_map/finish/pallas_call | solution.py:539

commit v3 on v2

--- a/solution.py
+++ b/solution.py
@@ -43,7 +43,8 @@
 
 
 def down_shares(chips, chunks):
-    return [max(chunks - (3 * chunks * q * q) // (4 * max(chips - 2, 1) ** 2), 0) for q in range(chips - 1)]
+    rise = [(3 * chunks * q * q) // (4 * max(chips - 2, 1) ** 2) for q in range(chips - 1)]
+    return [chunks - min(max(up, min(q, 1)), chunks) for q, up in enumerate(rise)]
 
 
 def kernel(
@@ -96,15 +97,6 @@
         peers = jnp.where(me >= distance, 1, 0) + jnp.where(me + distance < n, 1, 0)
         pl.semaphore_wait(semaphore, peers)
 
-    signal(barrier, 1)
-    rounds = distances(n)
-
-    def turn(i):
-        if 0 < i <= len(rounds):
-            await_signals(near_sem.at[i - 1], rounds[i - 1])
-        if i < len(rounds):
-            signal(near_sem.at[i], rounds[i])
-
     def fields(l, sem, start=0, stop=height):
         rows = pl.ds(start, stop - start)
         return (
@@ -125,71 +117,6 @@
 
     def cells(l, sem):
         return k_of(0, 3, l, sem), act_of(l, sem), code_of(0, 3, l, sem)
-
-    def start_layer(l, sem):
-        for copy in fields(l, sem) + cells(l, sem):
-            copy.start()
-
-    def await_planes(planes, rank, sem, rows=height):
-        ref = pa.at[pl.ds(0, planes), pl.ds(0, rank), pl.ds(0, rows)]
-        pltpu.make_async_copy(ref, ref, sem).wait()
-
-    def layer_sem(l):
-        return load_sem.at[l + 2]
-
-
-    def chunk_rows(c):
-        return pl.ds(pl.multiple_of(c * CHUNK, CHUNK), CHUNK)
-
-    def down(c, planes, kind):
-        rows = chunk_rows(c)
-        return pltpu.make_async_remote_copy(
-            src_ref=pa.at[pl.ds(0, planes), 0, rows], dst_ref=halo_t.at[pl.ds(0, planes), rows],
-            send_sem=sems.at[kind], recv_sem=chunk_recv.at[c], device_id={"gx": lower}, device_id_type=MESH)
-
-    def up(c, planes, kind):
-        rows = chunk_rows(c)
-        return pltpu.make_async_remote_copy(
-            src_ref=pa.at[pl.ds(0, planes), last, rows], dst_ref=halo_b.at[pl.ds(0, planes), rows],
-            send_sem=sems.at[kind], recv_sem=chunk_recv.at[c], device_id={"gx": upper}, device_id_type=MESH)
-
-    def back_up(c, kind):
-        rows = chunk_rows(c)
-        return pltpu.make_async_remote_copy(
-            src_ref=ret_t_out.at[rows], dst_ref=ret_b_in.at[rows],
-            send_sem=sems.at[BACK_SEND], recv_sem=sems.at[kind], device_id={"gx": upper}, device_id_type=MESH)
-
-    def back_down(c, kind):
-        rows = chunk_rows(c)
-        return pltpu.make_async_remote_copy(
-            src_ref=ret_b_out.at[rows], dst_ref=ret_t_in.at[rows],
-            send_sem=sems.at[BACK_SEND], recv_sem=sems.at[kind], device_id={"gx": lower}, device_id_type=MESH)
-
-    D, DL, U, UL = 2 * steps + 1, 2 * steps + 2, 2 * steps + 2, 2 * steps + 3
-
-    pair = pltpu.make_async_remote_copy(
-        src_ref=pa.at[pl.ds(0, D), 0, pl.ds(0, height)], dst_ref=halo_t.at[pl.ds(0, D)],
-        send_sem=sems.at[PAIR_SEND], recv_sem=sems.at[PAIR], device_id={"gx": lower}, device_id_type=MESH)
-    pair_back = pltpu.make_async_remote_copy(
-        src_ref=ret_t_out, dst_ref=ret_b_in,
-        send_sem=sems.at[PAIR_SEND], recv_sem=sems.at[PAIR_BACK], device_id={"gx": upper}, device_id_type=MESH)
-
-    def await_bytes(ref, sem):
-        pltpu.make_async_copy(ref, ref, sems.at[sem]).wait()
-
-    def await_rows(ref, count, sem):
-        if count > 0:
-            await_bytes(ref.at[pl.ds(0, count * CHUNK)], sem)
-
-    def await_planes_of(ref, planes, count, sem):
-        if count > 0:
-            await_bytes(ref.at[pl.ds(0, planes), pl.ds(0, count * CHUNK)], sem)
-
-    def each_share(side, body):
-        for value in sorted(set(shares)):
-            @pl.when(jnp.logical_and(jnp.logical_and(apart, side), share == value))
-            def _(value=value):
-                body(value, max(value - LATE, 0), max(chunks - LATE, value))
 
     head = HEAD * CHUNK
     load_k = pltpu.make_async_copy(k_hbm.at[0, last], pa.at[K, last, pl.ds(0, height)], load_sem.at[2])
@@ -199,6 +126,80 @@
         + (load_k, act_of(last, load_sem.at[2]), code_of(0, 1, last, load_sem.at[2])) + fields(last, load_sem.at[2])
     ):
         copy.start()
+
+    signal(barrier, 1)
+    rounds = distances(n)
+
+    def turn(i):
+        if 0 < i <= len(rounds):
+            await_signals(near_sem.at[i - 1], rounds[i - 1])
+        if i < len(rounds):
+            signal(near_sem.at[i], rounds[i])
+
+    def start_layer(l, sem):
+        for copy in fields(l, sem) + cells(l, sem):
+            copy.start()
+
+    def await_planes(planes, rank, sem, rows=height):
+        ref = pa.at[pl.ds(0, planes), pl.ds(0, rank), pl.ds(0, rows)]
+        pltpu.make_async_copy(ref, ref, sem).wait()
+
+    def layer_sem(l):
+        return load_sem.at[l + 2]
+
+
+    def chunk_rows(c):
+        return pl.ds(pl.multiple_of(c * CHUNK, CHUNK), CHUNK)
+
+    def down(c, planes, kind):
+        rows = chunk_rows(c)
+        return pltpu.make_async_remote_copy(
+            src_ref=pa.at[pl.ds(0, planes), 0, rows], dst_ref=halo_t.at[pl.ds(0, planes), rows],
+            send_sem=sems.at[kind], recv_sem=chunk_recv.at[c], device_id={"gx": lower}, device_id_type=MESH)
+
+    def up(c, planes, kind):
+        rows = chunk_rows(c)
+        return pltpu.make_async_remote_copy(
+            src_ref=pa.at[pl.ds(0, planes), last, rows], dst_ref=halo_b.at[pl.ds(0, planes), rows],
+            send_sem=sems.at[kind], recv_sem=chunk_recv.at[c], device_id={"gx": upper}, device_id_type=MESH)
+
+    def back_up(c, kind):
+        rows = chunk_rows(c)
+        return pltpu.make_async_remote_copy(
+            src_ref=ret_t_out.at[rows], dst_ref=ret_b_in.at[rows],
+            send_sem=sems.at[BACK_SEND], recv_sem=sems.at[kind], device_id={"gx": upper}, device_id_type=MESH)
+
+    def back_down(c, kind):
+        rows = chunk_rows(c)
+        return pltpu.make_async_remote_copy(
+            src_ref=ret_b_out.at[rows], dst_ref=ret_t_in.at[rows],
+            send_sem=sems.at[BACK_SEND], recv_sem=sems.at[kind], device_id={"gx": lower}, device_id_type=MESH)
+
+    D, DL, U, UL = 2 * steps + 1, 2 * steps + 2, 2 * steps + 2, 2 * steps + 3
+
+    pair = pltpu.make_async_remote_copy(
+        src_ref=pa.at[pl.ds(0, D), 0, pl.ds(0, height)], dst_ref=halo_t.at[pl.ds(0, D)],
+        send_sem=sems.at[PAIR_SEND], recv_sem=sems.at[PAIR], device_id={"gx": lower}, device_id_type=MESH)
+    pair_back = pltpu.make_async_remote_copy(
+        src_ref=ret_t_out, dst_ref=ret_b_in,
+        send_sem=sems.at[PAIR_SEND], recv_sem=sems.at[PAIR_BACK], device_id={"gx": upper}, device_id_type=MESH)
+
+    def await_bytes(ref, sem):
+        pltpu.make_async_copy(ref, ref, sems.at[sem]).wait()
+
+    def await_rows(ref, count, sem):
+        if count > 0:
+            await_bytes(ref.at[pl.ds(0, count * CHUNK)], sem)
+
+    def await_planes_of(ref, planes, count, sem):
+        if count > 0:
+            await_bytes(ref.at[pl.ds(0, planes), pl.ds(0, count * CHUNK)], sem)
+
+    def each_share(side, body):
+        for value in sorted(set(shares)):
+            @pl.when(jnp.logical_and(jnp.logical_and(apart, side), share == value))
+            def _(value=value):
+                body(value, max(value - LATE, 0), max(chunks - LATE, value))
 
     tail[0:8] = jnp.zeros((8, width), jnp.float32)
 

time: 21.6 us -> 21.4 us (level)
  no operation moved by 1% of the time
where the time goes in v3:
time: 21.4 us; the launch traced here: 21.3 us
  Pallas kernels  21.3 us (100%)
    pallas_call x1, Pallas kernels, local(): pl.pallas_call(functools.partial(kernel, n), out_shape=(pltpu.VMEM((3, la...  20.1 us
    pallas_call x1, Pallas kernels, local(): pl.pallas_call(finish, out_shape=jax.ShapeDtypeStruct(raw.shape, f32), in...  1.13 us

profile of v3, /device:TPU:0, one launch (start us, length us, event | category | flops | bytes accessed | tf_op | source)
XLA Modules:
  0.0 21.3 jit_solution(11461940865256232043)
XLA Ops:
  0.0 20.1 %faces.1 = (f32[3,8,128,128]{3,2,1,0:T(8,128)S(1)}, f32[8,128]{1,0:T(8,128)S(1)}) custom-call(f32[7,8,128,128]{3,2,1,0:T(8,128)} %p_hbm.1, f32[7,8,128,128]{3,2,1,0:T(8,128)} %a_hbm.1, f32[3,8,128,128]{3,2,1,0:T(8,128)} %k_hbm.1, s32[8,128,128]{2,1,0:T(8,128)} %act_hbm.1, s32[3,8,128,128]{3,2,1,0:T(8,128)} %code_hbm.1), custom_call_target="tpu_custom_call" | custom-call | flops 100000000 | bytes 12000000 | tf_op jit(solution)/shard_map/faces/pallas_call | solution.py:512
  20.2 1.1 %finish.1 = f32[3,8,128,128]{3,2,1,0:T(8,128)} custom-call(f32[3,8,128,128]{3,2,1,0:T(8,128)S(1)} %get-tuple-element.7.raw, f32[8,128]{1,0:T(8,128)S(1)} %get-tuple-element.8.scale), custom_call_target="tpu_custom_call" | custom-call | tf_op jit(solution)/shard_map/finish/pallas_call | solution.py:540

commit v4 on v3

--- a/solution.py
+++ b/solution.py
@@ -232,7 +232,6 @@
     @pl.when(odd)
     def _():
         loop(share, late_up, lambda c: up(c, U, SEND).start())
-        pair.start()
 
     for copy in (
         k_of(1, 3, 0, load_sem.at[3]), code_of(0, 3, 0, load_sem.at[3]),
@@ -268,7 +267,6 @@
     await_planes(2 * steps - 1, 4, load_sem.at[3])
     cross(0)
     cross(last - 1)
-    turn(1)
     pa[OWN_UP, 0, 0:height] = grad[0, 0]
     pa[OWN_LO, last, 0:height] = grad[0, last]
 
@@ -279,6 +277,9 @@
     @pl.when(odd)
     def _():
         loop(late_up, rows_end, lambda c: up(c, UL, SEND_LATE).start())
+        pair.start()
+
+    turn(1)
 
     def lanes_weight(l, r, prod):
         here = pl.ds(r, ROWS)
@@ -397,7 +398,6 @@
     def top_late(c, total):
         down(c, DL, SEND_LATE).wait_recv()
         squares, w_up = face_top(chunk_rows(c), CHUNK)
-        back_up(c, BACK_LATE).start()
         return total + squares + fold(halo_t[OWN_UP, chunk_rows(c)] + w_up)
 
     def bottom_early(c, total):
@@ -409,7 +409,6 @@
     def bottom_late(c, total):
         up(c, UL, SEND_LATE).wait_recv()
         squares, w_lo = face_bottom(chunk_rows(c), CHUNK)
-        back_down(c, BACK_LATE).start()
         return total + squares + fold(halo_b[OWN_LO, chunk_rows(c)] + w_lo)
 
     def add_bottom(c, total):
@@ -456,6 +455,8 @@
 
     loop(0, me, lambda j: to_peer(j).start())
     loop(me + 1, n, lambda j: to_peer(j).start())
+    loop(when_odd(late_down), when_odd(share), lambda c: back_up(c, BACK_LATE).start())
+    loop(when_even(late_up), when_even(rows_end), lambda c: back_down(c, BACK_LATE).start())
     parts[me] = mine
 
     each_share(even, lambda value, below, above: await_rows(ret_b_in, value - below, BACK_LATE))

time: 21.4 us -> 21.4 us (level)
  no operation moved by 1% of the time
where the time goes in v4:
time: 21.4 us; the launch traced here: 21.3 us
  Pallas kernels  21.3 us (100%)
    pallas_call x1, Pallas kernels, local(): pl.pallas_call(functools.partial(kernel, n), out_shape=(pltpu.VMEM((3, la...  20.1 us
    pallas_call x1, Pallas kernels, local(): pl.pallas_call(finish, out_shape=jax.ShapeDtypeStruct(raw.shape, f32), in...  1.13 us

profile of v4, /device:TPU:0, one launch (start us, length us, event | category | flops | bytes accessed | tf_op | source)
XLA Modules:
  0.0 21.3 jit_solution(16579021455524219466)
XLA Ops:
  0.0 20.1 %faces.1 = (f32[3,8,128,128]{3,2,1,0:T(8,128)S(1)}, f32[8,128]{1,0:T(8,128)S(1)}) custom-call(f32[7,8,128,128]{3,2,1,0:T(8,128)} %p_hbm.1, f32[7,8,128,128]{3,2,1,0:T(8,128)} %a_hbm.1, f32[3,8,128,128]{3,2,1,0:T(8,128)} %k_hbm.1, s32[8,128,128]{2,1,0:T(8,128)} %act_hbm.1, s32[3,8,128,128]{3,2,1,0:T(8,128)} %code_hbm.1), custom_call_target="tpu_custom_call" | custom-call | flops 100000000 | bytes 12000000 | tf_op jit(solution)/shard_map/faces/pallas_call | solution.py:513
  20.1 1.1 %finish.1 = f32[3,8,128,128]{3,2,1,0:T(8,128)} custom-call(f32[3,8,128,128]{3,2,1,0:T(8,128)S(1)} %get-tuple-element.7.raw, f32[8,128]{1,0:T(8,128)S(1)} %get-tuple-element.8.scale), custom_call_target="tpu_custom_call" | custom-call | tf_op jit(solution)/shard_map/finish/pallas_call | solution.py:541

commit v5 on v4

--- a/solution.py
+++ b/solution.py
@@ -12,7 +12,7 @@
 ROWS = 64
 CHUNK = 8
 LATE = 4
-HEAD = 2
+HEAD = 1
 PAD = 8
 GRANT = 58_000_000
 
@@ -213,13 +213,14 @@
 
     await_signals(barrier, 1)
     await_planes(8, 1, load_sem.at[0], (2 * steps * head + 2 * height) // 8)
-    pa[K, 0, 0:height] = k[0, 0, 0:height] * act[0, 0:height].astype(jnp.float32)
+    pa[K, 0, 0:head] = k[0, 0, 0:head] * act[0, 0:head].astype(jnp.float32)
     ahead = jnp.where(late_down < HEAD, late_down, HEAD)
 
     @pl.when(even)
     def _():
         loop(0, ahead, lambda c: down(c, D, SEND).start())
 
+    pa[K, 0, head:height] = k[0, 0, head:height] * act[0, head:height].astype(jnp.float32)
     await_planes(2 * steps, 1, load_sem.at[1], height - head)
 
     @pl.when(even)

time: 21.4 us -> 21.4 us (level)
  no operation moved by 1% of the time
where the time goes in v5:
time: 21.4 us; the launch traced here: 21.2 us
  Pallas kernels  21.2 us (99%)
    pallas_call x1, Pallas kernels, local(): pl.pallas_call(functools.partial(kernel, n), out_shape=(pltpu.VMEM((3, la...  20.1 us
    pallas_call x1, Pallas kernels, local(): pl.pallas_call(finish, out_shape=jax.ShapeDtypeStruct(raw.shape, f32), in...  1.13 us

profile of v5, /device:TPU:0, one launch (start us, length us, event | category | flops | bytes accessed | tf_op | source)
XLA Modules:
  0.0 21.2 jit_solution(9530494934309743146)
XLA Ops:
  0.0 20.1 %faces.1 = (f32[3,8,128,128]{3,2,1,0:T(8,128)S(1)}, f32[8,128]{1,0:T(8,128)S(1)}) custom-call(f32[7,8,128,128]{3,2,1,0:T(8,128)} %p_hbm.1, f32[7,8,128,128]{3,2,1,0:T(8,128)} %a_hbm.1, f32[3,8,128,128]{3,2,1,0:T(8,128)} %k_hbm.1, s32[8,128,128]{2,1,0:T(8,128)} %act_hbm.1, s32[3,8,128,128]{3,2,1,0:T(8,128)} %code_hbm.1), custom_call_target="tpu_custom_call" | custom-call | flops 100000000 | bytes 12000000 | tf_op jit(solution)/shard_map/faces/pallas_call | solution.py:514
  20.1 1.1 %finish.1 = f32[3,8,128,128]{3,2,1,0:T(8,128)} custom-call(f32[3,8,128,128]{3,2,1,0:T(8,128)S(1)} %get-tuple-element.7.raw, f32[8,128]{1,0:T(8,128)S(1)} %get-tuple-element.8.scale), custom_call_target="tpu_custom_call" | custom-call | tf_op jit(solution)/shard_map/finish/pallas_call | solution.py:542
